TPU v7x, 32 devices: a whole 2x2x4 slice. The times are simulated.
32 devices in a mesh: sub: 16 (over z, x, core), chan: 2 (over y).
Axes of the slice: x: 2, y: 2, z: 4, core: 2. Of those that a mesh axis runs over, the one named last changes fastest.
Arguments:
- raw_pulses: bfloat16 [2, 512, 2, 2048], P(None, 'sub', 'chan'), may hold values from -6 to 6
- range_filter: bfloat16 [2, 2048, 1024], P(None, ('sub', 'chan')), may hold values from -0.09375 to 0.09375
- channel_mix: float32 [2, 32, 2, 2], replicated, may hold values from -3 to 3
- steer_angles: float32 [256], replicated, may hold values from -3.140625 to 3.140625
- band_offsets: int32 [4, 512], replicated, may hold values from 0 to 248
- band_weights: float32 [4, 2, 2, 512, 8], replicated, may hold values from -1 to 1
- smoothing: float32 [4096], P('sub'), may hold values from 0.3 to 0.5
Outputs:
- despeckled: float32 [4096, 1024], P('sub', 'chan')
All inputs are finite; a program needn't handle non-finite values.
Results may differ from a plain program's by a relative error of at most 0.0036.
Values may be sent and summed in bfloat16 or wider, within the bound.
A program may use at most 64 MiB of HBM per device.

v0:
```python
import jax
import jax.numpy as jnp
import numpy as np
from jax import lax
from jax.experimental import pallas as pl
from jax.sharding import PartitionSpec as P

PASSES = 3
HIGH = lax.Precision.HIGHEST
LOW = jnp.bfloat16


def rounded(value):
    return lax.reduce_precision(value, exponent_bits=8, mantissa_bits=7)


def halves(value):
    top = rounded(value)
    return top.astype(LOW), (value - top).astype(LOW)


def doppler_table(count):
    index_row = jnp.arange(count, dtype=jnp.int32)
    product = index_row[:, None] * index_row[None, :] % count
    phase = 2.0 * np.pi / count * product.astype(jnp.float32)
    factor = 1.0 / np.sqrt(count)
    return (
        rounded(jnp.cos(phase) * factor),
        rounded(-jnp.sin(phase) * factor),
    )


def steer_table(steer_angles, count):
    offsets = jnp.arange(count, dtype=jnp.int32).astype(jnp.float32) - 0.5 * count
    phase = offsets[:, None] * steer_angles[None, :]
    factor = 1.0 / np.sqrt(count)
    return (
        rounded(jnp.cos(phase) * factor),
        rounded(jnp.sin(phase) * factor),
    )


def forming_operator(channel_mix, steer_angles, pulse_count):
    channels = channel_mix.shape[2]
    dop_r, dop_i = doppler_table(pulse_count)
    beam_r, beam_i = steer_table(steer_angles, channels * pulse_count)
    mix = channel_mix.transpose(0, 3, 2, 1)[:, :, None, :, :]
    dr, di = dop_r.T[None, :, None, :], dop_i.T[None, :, None, :]
    shape = (channels * pulse_count, channels * pulse_count)
    mixed_r = (mix[0] * dr - mix[1] * di).reshape(shape)
    mixed_i = (mix[0] * di + mix[1] * dr).reshape(shape)
    left = jnp.concatenate([mixed_r, mixed_i], axis=1)
    t_r = jnp.dot(left, jnp.concatenate([beam_r, -beam_i], axis=0), precision=HIGH)
    t_i = jnp.dot(left, jnp.concatenate([beam_i, beam_r], axis=0), precision=HIGH)
    angles = steer_angles.shape[0]
    t_r = t_r.reshape(channels, pulse_count, angles)
    t_i = t_i.reshape(channels, pulse_count, angles)
    top = jnp.concatenate([t_r, t_i], axis=2)
    low = jnp.concatenate([-t_i, t_r], axis=2)
    both = jnp.concatenate([top, low], axis=1)
    return both.reshape(channels * 2 * pulse_count, 2 * angles)


def operator_body(offsets_ref, weights_ref, *out_refs):
    band_width, count = weights_ref.shape[3], weights_ref.shape[4]
    delta = lax.broadcasted_iota(jnp.int32, (count, count), 0) - offsets_ref[0]
    bands = [jnp.zeros((count, count), jnp.float32)] * 2
    for j in range(band_width):
        hit = delta == j
        bands = [
            jnp.where(hit, weights_ref[0, 0, part, j : j + 1, :], bands[part]) for part in range(2)
        ]
    for order, ref in enumerate(out_refs):
        real, imag = (band.astype(LOW) for band in bands)
        ref[0, 0, :count, :count] = real
        ref[0, 0, :count, count:] = imag
        ref[0, 0, count:, :count] = -imag
        ref[0, 0, count:, count:] = real
        if order + 1 < len(out_refs):
            bands = [band - band.astype(LOW).astype(jnp.float32) for band in bands]


def merge_operators(offsets, weights, parts):
    levels, _, _, merged, band_width = weights.shape
    count = merged // 2
    by_step = weights.transpose(0, 1, 2, 4, 3)
    shape = jax.ShapeDtypeStruct((levels, 2, 2 * count, 2 * merged), LOW)
    return pl.pallas_call(
        operator_body,
        grid=(levels, 2, 2),
        in_specs=[
            pl.BlockSpec((1, 1, count), lambda l, c, h: (l, 0, h)),
            pl.BlockSpec((1, 1, 2, band_width, count), lambda l, c, h: (l, c, 0, 0, h)),
        ],
        out_specs=[
            pl.BlockSpec((1, 1, 2 * count, 2 * count), lambda l, c, h: (l, c, 0, h))
        ] * parts,
        out_shape=[shape] * parts,
        cost_estimate=pl.CostEstimate(
            flops=levels * 4 * count * count * 32,
            bytes_accessed=levels * parts * 16 * count * count * 2,
            transcendentals=0,
        ),
    )(offsets[:, None, :], by_step)


def low_dot(left, right):
    return jnp.dot(left, right, preferred_element_type=jnp.float32)


def local(
    raw_pulses, range_filter, channel_mix, steer_angles, band_offsets, band_weights, smoothing
):
    pulses = raw_pulses.shape[1]
    samples = raw_pulses.shape[3]
    bins = range_filter.shape[2]
    angles = steer_angles.shape[0]
    levels = band_offsets.shape[0]
    subs, chans = lax.axis_size("sub"), lax.axis_size("chan")
    own = bins // (subs * chans)

    part = lax.all_to_all(range_filter, "chan", split_axis=2, concat_axis=1, tiled=True)
    filt = lax.all_gather(part, "sub", axis=1, tiled=True)
    echo = lax.all_gather(raw_pulses[:, :, 0, :], "chan", axis=0)

    forming = forming_operator(channel_mix, steer_angles, pulses)
    form_top, form_low = halves(forming)
    base_top, base_low = merge_operators(band_offsets[:1], band_weights[:1], 2)
    folded = [
        low_dot(form_top, base_top[0, c])
        + (low_dot(form_low, base_top[0, c]) + low_dot(form_top, base_low[0, c]))
        for c in range(2)
    ]
    folded_top, folded_low = halves(jnp.concatenate(folded, axis=0))
    (later,) = merge_operators(band_offsets[1:], band_weights[1:], 1)

    real_rows = jnp.concatenate([echo[:, 0], -echo[:, 1]], axis=2)
    imag_rows = jnp.concatenate([echo[:, 1], echo[:, 0]], axis=2)
    stacked = jnp.concatenate([real_rows, imag_rows], axis=1).reshape(-1, 2 * samples)
    compressed = low_dot(stacked, filt.reshape(2 * samples, -1)).astype(LOW)
    blocks = compressed.T.reshape(subs, own, -1)
    got = lax.all_to_all(blocks, "sub", split_axis=0, concat_axis=0, tiled=True)
    image = got.reshape(subs * own, -1)
    for level in range(levels):
        run = (1 << level) * own
        wide = image.shape[1]
        field = image.astype(LOW).reshape(-1, 2, run, wide)
        pair = jnp.concatenate([field[:, 0], field[:, 1]], axis=2).reshape(-1, 2 * wide)
        if level == 0:
            out = low_dot(pair, folded_top) + low_dot(pair, folded_low)
        else:
            out = low_dot(pair, later[level - 1].reshape(2 * wide, -1))
        out = out.reshape(-1, run, 4 * angles)
        image = jnp.stack([out[:, :, : 2 * angles], out[:, :, 2 * angles :]], axis=1)
        image = image.reshape(-1, 2 * angles)
    power = image[:, :angles] * image[:, :angles] + image[:, angles:] * image[:, angles:]
    power = power.astype(LOW).reshape(subs, own, angles)
    power = lax.all_to_all(power, "sub", split_axis=0, concat_axis=0, tiled=True)
    power = power.reshape(subs * own, angles)
    up = [(i, i + 1) for i in range(chans - 1)]
    down = [(j, i) for i, j in up]
    before = lax.ppermute(power[-PASSES:], "chan", up).astype(jnp.float32)
    after = lax.ppermute(power[:PASSES], "chan", down).astype(jnp.float32)
    power = jnp.concatenate([before, power.astype(jnp.float32), after], axis=0)
    rate = smoothing[None, :]
    at = lax.axis_index("chan")
    lead, trail = at == 0, at == chans - 1
    for sweep in range(PASSES):
        mid = power[1:-1]
        power = mid + rate * (power[:-2] - 2.0 * mid + power[2:])
        edge = PASSES - 1 - sweep
        if edge:
            inner = power[edge:-edge]
            head = jnp.where(lead, 0.0, power[:edge])
            tail = jnp.where(trail, 0.0, power[-edge:])
            power = jnp.concatenate([head, inner, tail], axis=0)
    return power.T


def solution(mesh):
    in_specs = (
        P(None, "sub", "chan", None),
        P(None, ("sub", "chan"), None),
        P(),
        P(),
        P(),
        P(),
        P("sub"),
    )
    out_specs = P("sub", "chan")
    return jax.shard_map(local, mesh=mesh, in_specs=in_specs, out_specs=out_specs, check_vma=False)
```

profile of v0, /device:TPU:0, one launch (start us, length us, event | category | flops | bytes accessed | tf_op | source)
XLA Modules:
  0.0 119.9 jit_solution(8060832167545414871)
XLA Ops:
  6.5 1.3 %copy.42 = bf16[2,64,1024]{1,0,2:T(2,128)(2,1)S(1)} copy(bf16[2,64,1024]{2,1,0:T(8,128)(2,1)} %param.8) | data formatting | bytes 524288 | tf_op args[1]
  7.9 0.4 reshape.197
  8.3 9.2 %all_to_all.28 = bf16[2,2,32768]{2,1,0:T(2,128)(2,1)S(1)} all-to-all(bf16[2,2,32768]{2,1,0:T(2,128)(2,1)S(1)} %reshape.197), channel_id=1, replica_groups=mesh['sub'=16,'chan'=2] {'chan'}, dimensions={0} | all-to-all | bytes 524288 | tf_op jit(solution)/shard_map/all_to_all | solution.py:122
  17.5 0.3 reshape.198
  17.9 1.0 copy.44
  18.9 0.6 broadcast_in_dim.26.offsets_ref
  19.5 0.1 multiply_reduce-precision_fusion
  19.7 0.1 add.71
  19.8 0.1 sub.38
  19.9 0.3 fusion.51
  20.2 0.3 fusion.44
  20.5 0.6 slice_bitcast_fusion.18.offsets_ref
  21.1 0.6 slice_bitcast_fusion.17.weights_ref
  21.7 4.2 %shard_map.73 = (bf16[1,2,512,1024]{3,2,1,0:T(8,128)(2,1)}, bf16[1,2,512,1024]{3,2,1,0:T(8,128)(2,1)}) custom-call(s32[1,1,512]{2,1,0:T(1,128)} %slice_bitcast_fusion.18.offsets_ref, f32[1,2,2,8,512]{4,3,2,1,0:T(8,128)} %slice_bitcast_fusion.17.weights_ref), custom_call_target="tpu_custom_call" | custom-call | flops 8388608 | bytes 4194304 | tf_op jit(solution)/shard_map/pallas_call | solution.py:88
  25.9 0.7 slice_bitcast_fusion.16.weights_ref
  26.6 9.0 %shard_map.74 = bf16[3,2,512,1024]{3,2,1,0:T(8,128)(2,1)} custom-call(s32[3,1,512]{2,1,0:T(1,128)} %broadcast_in_dim.26.offsets_ref, f32[3,2,2,8,512]{4,3,2,1,0:T(8,128)} %slice_bitcast_fusion.16.weights_ref), custom_call_target="tpu_custom_call" | custom-call | flops 25165824 | bytes 6291456 | tf_op jit(solution)/shard_map/pallas_call | solution.py:88
  35.6 0.3 fusion.40
  35.9 7.4 %all-gather = bf16[4,32,1,2048]{3,1,2,0:T(8,128)(2,1)S(1)} all-gather(bf16[2,32,1,2048]{3,1,2,0:T(8,128)(2,1)S(1)} %copy-done.5), channel_id=2, replica_groups=mesh['sub'=16,'chan'=2] {'chan'}, dimensions={0}, use_global_device_ids=true | all-gather | bytes 786432 | tf_op jit(solution)/shard_map/all_gather | solution.py:124
  43.3 0.3 fusion.4
  43.6 0.3 fusion.8
  44.0 0.3 convolution_add_fusion.1
  44.3 0.3 convolution_add_fusion.2
  44.6 1.1 convolution_add_fusion.3
  45.7 1.7 %copy-done = bf16[3,2,512,1024]{3,2,1,0:T(8,128)(2,1)S(1)} copy-done((bf16[3,2,512,1024]{3,2,1,0:T(8,128)(2,1)S(1)}, bf16[3,2,512,1024]{3,2,1,0:T(8,128)(2,1)}, u32[]{:S(2)}) %copy-start) | copy-done | bytes 6291480
  47.5 3.0 %fusion.69 = (bf16[1,2,512,1024]{3,2,1,0:T(8,128)(2,1)}, bf16[1,2,512,1024]{3,2,1,0:T(8,128)(2,1)S(1)}, bf16[1,2,512,1024]{3,2,1,0:T(8,128)(2,1)}) fusion(bf16[3,2,512,1024]{3,2,1,0:T(8,128)(2,1)S(1)} %copy-done), kind=kLoop, calls=%fused_computation.136 | loop fusion | bytes 12582912 | tf_op jit(solution)/shard_map/slice | solution.py:152
  50.6 1.1 maximum_maximum_fusion
  51.7 18.1 %all-gather.3.cloned.1.call-done = bf16[2,2048,512]{2,1,0:T(8,128)(2,1)} async-done(((bf16[2,128,512]{2,1,0:T(8,128)(2,1)}), bf16[2,2048,512]{2,1,0:T(8,128)(2,1)}) %all-gather.3.cloned.1.call-update) | async-done | bytes 4194320 | tf_op jit(solution)/shard_map/all_gather | solution.py:123
  69.8 3.2 %fusion.1 = bf16[512,128]{0,1:T(8,128)(2,1)S(1)} fusion(bf16[128,4096]{1,0:T(8,128)(2,1)} %bitcast.132, bf16[4096,512]{1,0:T(8,128)(2,1)} %bitcast.131), kind=kOutput, calls=%fused_computation.12 | convolution fusion | flops 536936448 | bytes 5373952 | tf_op jit(solution)/shard_map/dot_general | solution.py:108
  73.1 0.7 copy.45
  73.8 3.5 %all-to-all-start.1 = ((bf16[16,32,128]{2,1,0:T(8,128)(2,1)}), bf16[16,32,128]{2,1,0:T(8,128)(2,1)S(1)}, u32[]{:S(2)}, u32[]{:S(2)}) async-start(bf16[16,32,128]{2,1,0:T(8,128)(2,1)} %bitcast.10), calls=%async_computation.1 | async-start | bytes 262144 | tf_op jit(solution)/shard_map/all_to_all | solution.py:142
  77.3 1.7 %convolution_add_fusion.4 = f32[128,1024]{1,0:T(8,128)S(1)} fusion(f32[128,1024]{1,0:T(8,128)} %convolution_add_fusion.3, bf16[128,512]{1,0:T(8,128)(2,1)S(1)} %bitcast.136, bf16[1,2,512,1024]{3,2,1,0:T(8,128)(2,1)} %get-tuple-element.7), kind=kOutput, calls=%fused_computation.10 | convolution fusion | flops 134348800 | bytes 2228224 | tf_op jit(solution)/shard_map/dot_general | solution.py:108
  79.0 6.2 %all-to-all-done.1 = bf16[16,32,128]{2,1,0:T(8,128)(2,1)S(1)} async-done(((bf16[16,32,128]{2,1,0:T(8,128)(2,1)}), bf16[16,32,128]{2,1,0:T(8,128)(2,1)S(1)}, u32[]{:S(2)}, u32[]{:S(2)}) %all-to-all-start.1) | async-done | bytes 131104 | tf_op jit(solution)/shard_map/all_to_all | solution.py:142
  85.2 0.3 fusion.23
  85.5 0.3 fusion
  86.0 1.4 %copy-done.4 = bf16[1,2,512,1024]{3,2,1,0:T(8,128)(2,1)S(1)} copy-done((bf16[1,2,512,1024]{3,2,1,0:T(8,128)(2,1)S(1)}, bf16[1,2,512,1024]{3,2,1,0:T(8,128)(2,1)}, u32[]{:S(2)}) %copy-start.4) | copy-done | bytes 2097176
  87.4 0.7 convolution_convert_fusion.1
  88.3 1.4 %copy-done.3 = bf16[1,2,512,1024]{3,2,1,0:T(8,128)(2,1)S(1)} copy-done((bf16[1,2,512,1024]{3,2,1,0:T(8,128)(2,1)S(1)}, bf16[1,2,512,1024]{3,2,1,0:T(8,128)(2,1)}, u32[]{:S(2)}) %copy-start.3) | copy-done | bytes 2097176
  89.7 0.7 convolution_convert_fusion
  90.6 0.7 convolution_bitcast_fusion
  91.4 0.1 slice_bitcast_fusion.1
  91.6 12.6 %all_to_all.29 = bf16[16,32,256]{2,1,0:T(8,128)(2,1)S(1)} all-to-all(bf16[16,32,256]{2,1,0:T(8,128)(2,1)S(1)} %bitcast.152), channel_id=1, replica_groups=mesh['sub'=16,'chan'=2] {'sub'}, dimensions={0} | all-to-all | bytes 524288 | tf_op jit(solution)/shard_map/all_to_all | solution.py:158
  104.2 1.3 %collective-permute-start.1 = (bf16[3,256]{1,0:T(4,128)(2,1)S(1)}, bf16[3,256]{1,0:T(4,128)(2,1)S(1)}, u32[]{:S(2)}, u32[]{:S(2)}) collective-permute-start(bf16[3,256]{1,0:T(4,128)(2,1)S(1)} %get-tuple-element.33), channel_id=1, source_target_pairs={{1,0},{3,2},{5,4},{7,6},{9,8},{11,10},{13,12},{15,14},{17,16},{19,... | collective-permute-start | bytes 4616 | tf_op jit(solution)/shard_map/ppermute | solution.py:163
  105.5 4.5 %collective-permute-start = (bf16[3,256]{1,0:T(4,128)(2,1)S(1)}, bf16[3,256]{1,0:T(4,128)(2,1)S(1)}, u32[]{:S(2)}, u32[]{:S(2)}) collective-permute-start(bf16[3,256]{1,0:T(4,128)(2,1)S(1)} %get-tuple-element.32), channel_id=1, source_target_pairs={{0,1},{2,3},{4,5},{6,7},{8,9},{10,11},{12,13},{14,15},{16,17},{18,... | collective-permute-start | bytes 4616 | tf_op jit(solution)/shard_map/ppermute | solution.py:162
  110.1 1.3 %collective-permute-done = bf16[3,256]{1,0:T(4,128)(2,1)S(1)} collective-permute-done((bf16[3,256]{1,0:T(4,128)(2,1)S(1)}, bf16[3,256]{1,0:T(4,128)(2,1)S(1)}, u32[]{:S(2)}, u32[]{:S(2)}) %collective-permute-start) | collective-permute-done | bytes 1568 | tf_op jit(solution)/shard_map/ppermute | solution.py:162
  111.4 0.2 fusion.18
  111.7 0.2 fusion.21
  111.9 0.2 fusion.27
  112.1 1.0 copy.57
  (51 shorter events, 1.0 us)
Async XLA Ops:
  6.5 12.4 %copy-start.7 = (s32[4,512]{1,0:T(4,128)S(1)}, s32[4,512]{1,0:T(4,128)}, u32[]{:S(2)}) copy-start(s32[4,512]{1,0:T(4,128)} %param.11) | copy-start | bytes 24580
  6.5 13.1 %copy-start.9 = (f32[2,32,2,2]{1,3,2,0:T(2,128)S(1)}, f32[2,32,2,2]{1,3,2,0:T(2,128)}, u32[]{:S(2)}) copy-start(f32[2,32,2,2]{1,3,2,0:T(2,128)} %param.9) | copy-start | bytes 3076
  6.5 13.4 %copy-start.10 = (f32[256]{0:T(256)S(1)}, f32[256]{0:T(256)}, u32[]{:S(2)}) copy-start(f32[256]{0:T(256)} %param.10) | copy-start | bytes 3076
  6.5 63.3 %all-gather.3.cloned.1.call-start = ((), (), s32[]{:S(2)}) async-start(), calls=%async_computation.3 | async-start | bytes 4456448 | tf_op jit(solution)/shard_map/all_gather | solution.py:123
  7.8 13.3 %copy-start.6 = (f32[4,2,2,512,8]{3,4,2,1,0:T(8,128)S(1)}, f32[4,2,2,512,8]{3,4,2,1,0:T(8,128)}, u32[]{:S(2)}) copy-start(f32[4,2,2,512,8]{3,4,2,1,0:T(8,128)} %param.12) | copy-start | bytes 786436
  26.6 9.3 %copy-start.5 = (bf16[2,32,1,2048]{3,1,2,0:T(8,128)(2,1)S(1)}, bf16[2,32,1,2048]{3,1,2,0:T(8,128)(2,1)}, u32[]{:S(2)}) copy-start(bf16[2,32,1,2048]{3,1,2,0:T(8,128)(2,1)} %param.7) | copy-start | bytes 786436
  26.6 16.7 %copy-start.1 = (bf16[1,2,512,1024]{3,2,1,0:T(8,128)(2,1)S(1)}, bf16[1,2,512,1024]{3,2,1,0:T(8,128)(2,1)}, u32[]{:S(2)}) copy-start(bf16[1,2,512,1024]{3,2,1,0:T(8,128)(2,1)} %get-tuple-element.7) | copy-start | bytes 6291460
  35.9 8.0 %copy-start.2 = (bf16[1,2,512,1024]{3,2,1,0:T(8,128)(2,1)S(1)}, bf16[1,2,512,1024]{3,2,1,0:T(8,128)(2,1)}, u32[]{:S(2)}) copy-start(bf16[1,2,512,1024]{3,2,1,0:T(8,128)(2,1)} %get-tuple-element.8) | copy-start | bytes 6291460
  44.0 3.5 %copy-start = (bf16[3,2,512,1024]{3,2,1,0:T(8,128)(2,1)S(1)}, bf16[3,2,512,1024]{3,2,1,0:T(8,128)(2,1)}, u32[]{:S(2)}) copy-start(bf16[3,2,512,1024]{3,2,1,0:T(8,128)(2,1)} %shard_map.74) | copy-start | bytes 18874372
  73.8 11.4 %all-to-all-start.1 = ((bf16[16,32,128]{2,1,0:T(8,128)(2,1)}), bf16[16,32,128]{2,1,0:T(8,128)(2,1)S(1)}, u32[]{:S(2)}, u32[]{:S(2)}) async-start(bf16[16,32,128]{2,1,0:T(8,128)(2,1)} %bitcast.10), calls=%async_computation.1 | async-start | bytes 262144 | tf_op jit(solution)/shard_map/all_to_all | solution.py:142
  85.8 1.6 %copy-start.4 = (bf16[1,2,512,1024]{3,2,1,0:T(8,128)(2,1)S(1)}, bf16[1,2,512,1024]{3,2,1,0:T(8,128)(2,1)}, u32[]{:S(2)}) copy-start(bf16[1,2,512,1024]{3,2,1,0:T(8,128)(2,1)} %get-tuple-element.9) | copy-start | bytes 6291460
  88.1 1.6 %copy-start.3 = (bf16[1,2,512,1024]{3,2,1,0:T(8,128)(2,1)S(1)}, bf16[1,2,512,1024]{3,2,1,0:T(8,128)(2,1)}, u32[]{:S(2)}) copy-start(bf16[1,2,512,1024]{3,2,1,0:T(8,128)(2,1)} %get-tuple-element.11) | copy-start | bytes 6291460
  91.4 20.0 %copy-start.8 = (f32[256]{0:T(256)S(1)}, f32[256]{0:T(256)}, u32[]{:S(2)}) copy-start(f32[256]{0:T(256)} %param.13) | copy-start | bytes 3076
  104.2 5.8 %collective-permute-start.1 = (bf16[3,256]{1,0:T(4,128)(2,1)S(1)}, bf16[3,256]{1,0:T(4,128)(2,1)S(1)}, u32[]{:S(2)}, u32[]{:S(2)}) collective-permute-start(bf16[3,256]{1,0:T(4,128)(2,1)S(1)} %get-tuple-element.33), channel_id=1, source_target_pairs={{1,0},{3,2},{5,4},{7,6},{9,8},{11,10},{13,12},{15,14},{17,16},{19,... | collective-permute-start | bytes 4616 | tf_op jit(solution)/shard_map/ppermute | solution.py:163
  105.5 5.8 %collective-permute-start = (bf16[3,256]{1,0:T(4,128)(2,1)S(1)}, bf16[3,256]{1,0:T(4,128)(2,1)S(1)}, u32[]{:S(2)}, u32[]{:S(2)}) collective-permute-start(bf16[3,256]{1,0:T(4,128)(2,1)S(1)} %get-tuple-element.32), channel_id=1, source_target_pairs={{0,1},{2,3},{4,5},{6,7},{8,9},{10,11},{12,13},{14,15},{16,17},{18,... | collective-permute-start | bytes 4616 | tf_op jit(solution)/shard_map/ppermute | solution.py:162
Sparse Core Ops, SparseCore 0:
  19.0 50.7 all-gather.2
where the time goes:
time: 121 us; the launch traced here: 120 us
  blocking collectives  29.3 us (24%)
  waiting for transfers between devices  25.6 us (21%)
  local copies, waits for them, and re-layouts  15.7 us (13%)
  between operations  13.9 us (11%)
  Pallas kernels  13.2 us (11%)
  matrix products  10.5 us (9%)
  starting transfers between devices  9.33 us (8%)
  other arithmetic  2.48 us (2%)
    all_gather x1, waiting for transfers between devices, local(): filt = lax.all_gather(part, 'sub', axis=1, tiled=True)  18.1 us
    pallas_call x2, Pallas kernels, merge_operators(): pl.pallas_call(operator_body, grid=(levels, 2, 2), in_specs=[pl.BlockSpec...  13.2 us
    all_to_all x1, blocking collectives, local(): lax.all_to_all(power, 'sub', split_axis=0, concat_axis=0, tiled=True)  12.6 us
    dot_general x12, matrix products, low_dot(): return jnp.dot(left, right, preferred_element_type=jnp.float32)  9.98 us
    all_to_all x1, blocking collectives, local(): lax.all_to_all(range_filter, 'chan', split_axis=2, concat_axis=1, tiled=T...  9.24 us
    all_gather x1, blocking collectives, local(): echo = lax.all_gather(raw_pulses[:, :, 0, :], 'chan', axis=0)  7.41 us
    unnamed x25, local copies, waits for them, and re-layouts  6.64 us
    all_to_all x1, waiting for transfers between devices, local(): got = lax.all_to_all(blocks, 'sub', split_axis=0, concat_axis=0, tiled=True)  6.19 us
  transfers between devices with their start and end apart: 4, of which 3 were waited for; matrix products, arithmetic and copies ran while one was open for 10% of the time, Pallas kernels for 11%

commit v1 on v0

--- a/solution.py
+++ b/solution.py
@@ -3,7 +3,7 @@
 import numpy as np
 from jax import lax
 from jax.experimental import pallas as pl
-from jax.sharding import PartitionSpec as P
+from jax.sharding import Mesh, PartitionSpec as P
 
 PASSES = 3
 HIGH = lax.Precision.HIGHEST
@@ -116,12 +116,16 @@
     bins = range_filter.shape[2]
     angles = steer_angles.shape[0]
     levels = band_offsets.shape[0]
-    subs, chans = lax.axis_size("sub"), lax.axis_size("chan")
+    pairs, cores, chans = (lax.axis_size(name) for name in ("pair", "core", "chan"))
+    subs = pairs * cores
     own = bins // (subs * chans)
 
-    part = lax.all_to_all(range_filter, "chan", split_axis=2, concat_axis=1, tiled=True)
-    filt = lax.all_gather(part, "sub", axis=1, tiled=True)
-    echo = lax.all_gather(raw_pulses[:, :, 0, :], "chan", axis=0)
+    near = ("core", "chan")
+    split = range_filter.reshape(2, -1, chans, cores, pairs * own).swapaxes(2, 3)
+    split = split.reshape(range_filter.shape)
+    part = lax.all_to_all(split, near, split_axis=2, concat_axis=1, tiled=True)
+    filt = lax.all_gather(part, "pair", axis=1, tiled=True)
+    echo = lax.all_gather(raw_pulses[:, :, 0, :], near, axis=0)
 
     forming = forming_operator(channel_mix, steer_angles, pulses)
     form_top, form_low = halves(forming)
@@ -138,25 +142,25 @@
     imag_rows = jnp.concatenate([echo[:, 1], echo[:, 0]], axis=2)
     stacked = jnp.concatenate([real_rows, imag_rows], axis=1).reshape(-1, 2 * samples)
     compressed = low_dot(stacked, filt.reshape(2 * samples, -1)).astype(LOW)
-    blocks = compressed.T.reshape(subs, own, -1)
-    got = lax.all_to_all(blocks, "sub", split_axis=0, concat_axis=0, tiled=True)
-    image = got.reshape(subs * own, -1)
+    blocks = compressed.T.reshape(pairs, own, -1)
+    got = lax.all_to_all(blocks, "pair", split_axis=0, concat_axis=0, tiled=True)
     for level in range(levels):
         run = (1 << level) * own
-        wide = image.shape[1]
-        field = image.astype(LOW).reshape(-1, 2, run, wide)
-        pair = jnp.concatenate([field[:, 0], field[:, 1]], axis=2).reshape(-1, 2 * wide)
         if level == 0:
+            pair = got.reshape(pairs * own, -1)
             out = low_dot(pair, folded_top) + low_dot(pair, folded_low)
         else:
+            wide = image.shape[1]
+            field = image.astype(LOW).reshape(-1, 2, run, wide)
+            pair = jnp.concatenate([field[:, 0], field[:, 1]], axis=2).reshape(-1, 2 * wide)
             out = low_dot(pair, later[level - 1].reshape(2 * wide, -1))
         out = out.reshape(-1, run, 4 * angles)
         image = jnp.stack([out[:, :, : 2 * angles], out[:, :, 2 * angles :]], axis=1)
         image = image.reshape(-1, 2 * angles)
     power = image[:, :angles] * image[:, :angles] + image[:, angles:] * image[:, angles:]
     power = power.astype(LOW).reshape(subs, own, angles)
-    power = lax.all_to_all(power, "sub", split_axis=0, concat_axis=0, tiled=True)
-    power = power.reshape(subs * own, angles)
+    power = lax.all_to_all(power, ("pair", "core"), split_axis=0, concat_axis=0, tiled=True)
+    power = power.reshape(pairs, cores, own, angles).swapaxes(0, 1).reshape(subs * own, angles)
     up = [(i, i + 1) for i in range(chans - 1)]
     down = [(j, i) for i, j in up]
     before = lax.ppermute(power[-PASSES:], "chan", up).astype(jnp.float32)
@@ -178,14 +182,19 @@
 
 
 def solution(mesh):
+    devices = mesh.devices
+    grid = devices.reshape(devices.shape[0] // 2, 2, devices.shape[1])
+    split_mesh = Mesh(grid, ("pair", "core", "chan"))
+    sub = ("pair", "core")
     in_specs = (
-        P(None, "sub", "chan", None),
-        P(None, ("sub", "chan"), None),
-        P(),
-        P(),
-        P(),
-        P(),
-        P("sub"),
-    )
-    out_specs = P("sub", "chan")
-    return jax.shard_map(local, mesh=mesh, in_specs=in_specs, out_specs=out_specs, check_vma=False)
+        P(None, sub, "chan", None),
+        P(None, ("pair", "core", "chan"), None),
+        P(),
+        P(),
+        P(),
+        P(),
+        P(sub),
+    )
+    return jax.shard_map(
+        local, mesh=split_mesh, in_specs=in_specs, out_specs=P(sub, "chan"), check_vma=False
+    )

time: 121 us -> 131 us (1.083)
  waiting for transfers between devices: 25.6 us -> 45.1 us
  blocking collectives: 29.3 us -> 12.6 us
  starting transfers between devices: 9.33 us -> 13.5 us
  local copies, waits for them, and re-layouts: 15.7 us -> 19.4 us
    all_gather x1 -> x2, waiting for transfers between devices: 18.1 us -> 37.4 us  [the longest x1 37.4 us: local(): filt = lax.all_gather(part, 'pair', axis=1, tiled=True)]
    all_to_all x2 -> x1, blocking collectives: 21.9 us -> 12.6 us  [local(): lax.all_to_all(power, ('pair', 'core'), split_axis=0, concat_axis=0, tile...]
    all_gather x1 -> x0, blocking collectives: 7.41 us -> none  [local(): echo = lax.all_gather(raw_pulses[:, :, 0, :], 'chan', axis=0)]
    all_to_all x1 -> x2, starting transfers between devices: 3.51 us -> 7.64 us  [the longest x1 4.26 us: local(): part = lax.all_to_all(split, near, split_axis=2, concat_axis=1, tiled=True)]
    reshape x0 -> x2, local copies, waits for them, and re-layouts: none -> 1.65 us  [the longest x1 1.15 us: local(): range_filter.reshape(2, -1, chans, cores, pairs * own).swapaxes(2, 3)]
    unnamed x25 -> x24, local copies, waits for them, and re-layouts: 6.64 us -> 8.15 us
    all_to_all x1 -> x2, waiting for transfers between devices: 6.19 us -> 5.74 us  [the longest x1 5.74 us: local(): lax.all_to_all(blocks, 'pair', split_axis=0, concat_axis=0, tiled=True)]
  transfers between devices with their start and end apart: 4 -> 6, of which waited for: 3 -> 3; matrix products, arithmetic and copies ran while one was open for 10% -> 13% of each run, Pallas kernels for 11% -> 10%
where the time goes in v1:
time: 131 us; the launch traced here: 130 us
  waiting for transfers between devices  45.1 us (34%)
  local copies, waits for them, and re-layouts  19.4 us (15%)
  between operations  13.9 us (11%)
  starting transfers between devices  13.5 us (10%)
  Pallas kernels  13 us (10%)
  blocking collectives  12.6 us (10%)
  matrix products  9.53 us (7%)
  other arithmetic  2.59 us (2%)
    all_gather x1, waiting for transfers between devices, local(): filt = lax.all_gather(part, 'pair', axis=1, tiled=True)  37.4 us
    pallas_call x2, Pallas kernels, merge_operators(): pl.pallas_call(operator_body, grid=(levels, 2, 2), in_specs=[pl.BlockSpec...  13 us
    all_to_all x1, blocking collectives, local(): lax.all_to_all(power, ('pair', 'core'), split_axis=0, concat_axis=0, tile...  12.6 us
    dot_general x12, matrix products, low_dot(): return jnp.dot(left, right, preferred_element_type=jnp.float32)  9.01 us
    unnamed x24, local copies, waits for them, and re-layouts  8.15 us
    all_to_all x1, waiting for transfers between devices, local(): lax.all_to_all(blocks, 'pair', split_axis=0, concat_axis=0, tiled=True)  5.74 us
    ppermute x1, starting transfers between devices, local(): before = lax.ppermute(power[-PASSES:], 'chan', up).astype(jnp.float32)  4.54 us
    all_to_all x1, starting transfers between devices, local(): part = lax.all_to_all(split, near, split_axis=2, concat_axis=1, tiled=True)  4.26 us
  transfers between devices with their start and end apart: 6, of which 3 were waited for; matrix products, arithmetic and copies ran while one was open for 13% of the time, Pallas kernels for 10%

profile of v1, /device:TPU:0, one launch (start us, length us, event | category | flops | bytes accessed | tf_op | source)
XLA Modules:
  0.0 129.6 jit_solution(3758611117126286008)
XLA Ops:
  6.6 0.7 all-gather.6.cloned.1.call-update
  7.3 1.1 reshape.190
  8.4 0.5 copy.55
  8.9 1.1 reshape.208
  10.0 4.3 %all-to-all-start = ((bf16[4,2,16384]{2,1,0:T(2,128)(2,1)}), bf16[4,2,16384]{2,1,0:T(2,128)(2,1)S(1)}, u32[]{:S(2)}, u32[]{:S(2)}) async-start(bf16[4,2,16384]{2,1,0:T(2,128)(2,1)} %reshape.208), calls=%async_computation | async-start | bytes 524288 | tf_op jit(solution)/shard_map/all_to_all | solution.py:126
  14.4 0.6 broadcast_in_dim.26.offsets_ref
  15.3 0.3 fusion.50
  15.6 0.3 fusion.43
  15.9 0.6 slice_bitcast_fusion.17.weights_ref
  16.5 0.6 slice_bitcast_fusion.18.offsets_ref
  17.1 4.2 %shard_map.73 = (bf16[1,2,512,1024]{3,2,1,0:T(8,128)(2,1)}, bf16[1,2,512,1024]{3,2,1,0:T(8,128)(2,1)}) custom-call(s32[1,1,512]{2,1,0:T(1,128)} %slice_bitcast_fusion.18.offsets_ref, f32[1,2,2,8,512]{4,3,2,1,0:T(8,128)} %slice_bitcast_fusion.17.weights_ref), custom_call_target="tpu_custom_call" | custom-call | flops 8388608 | bytes 4194304 | tf_op jit(solution)/shard_map/pallas_call | solution.py:88
  21.3 0.3 reshape.209
  21.6 0.5 copy.56
  22.1 0.7 copy.43
  22.9 0.7 slice_bitcast_fusion.16.weights_ref
  23.5 8.9 %shard_map.74 = bf16[3,2,512,1024]{3,2,1,0:T(8,128)(2,1)} custom-call(s32[3,1,512]{2,1,0:T(1,128)} %broadcast_in_dim.26.offsets_ref, f32[3,2,2,8,512]{4,3,2,1,0:T(8,128)} %slice_bitcast_fusion.16.weights_ref), custom_call_target="tpu_custom_call" | custom-call | flops 25165824 | bytes 6291456 | tf_op jit(solution)/shard_map/pallas_call | solution.py:88
  32.4 0.3 fusion.39
  32.8 0.3 fusion.3
  33.1 0.3 fusion.7
  33.4 0.6 copy-done.3
  34.0 0.3 convolution_add_fusion.1
  34.4 0.3 convolution_add_fusion.2
  34.7 0.3 convolution_add_fusion.3
  35.0 1.8 %copy-done = bf16[3,2,512,1024]{3,2,1,0:T(8,128)(2,1)S(1)} copy-done((bf16[3,2,512,1024]{3,2,1,0:T(8,128)(2,1)S(1)}, bf16[3,2,512,1024]{3,2,1,0:T(8,128)(2,1)}, u32[]{:S(2)}) %copy-start) | copy-done | bytes 6291480
  36.8 2.9 %fusion.66 = (bf16[1,2,512,1024]{3,2,1,0:T(8,128)(2,1)}, bf16[1,2,512,1024]{3,2,1,0:T(8,128)(2,1)}, bf16[1,2,512,1024]{3,2,1,0:T(8,128)(2,1)}) fusion(bf16[3,2,512,1024]{3,2,1,0:T(8,128)(2,1)S(1)} %copy-done), kind=kLoop, calls=%fused_computation.132 | loop fusion | bytes 12582912 | tf_op jit(solution)/shard_map/slice | solution.py:156
  39.7 1.1 fusion.65
  40.8 1.3 %slice_bitcast_fusion.2 = (bf16[4,32,2048]{2,1,0:T(8,128)(2,1)S(1)}, bf16[4,32,2048]{2,1,0:T(8,128)(2,1)S(1)}) fusion(bf16[4,2,32,2048]{3,2,1,0:T(8,128)(2,1)} %bitcast.137), kind=kLoop, calls=%fused_computation.54 | loop fusion | bytes 2097152 | tf_op jit(solution)/shard_map/squeeze | solution.py:141
  42.3 37.4 %all-gather.4.cloned.1.call-done = bf16[2,2048,256]{2,1,0:T(8,128)(2,1)} async-done(((bf16[2,256,256]{2,1,0:T(8,128)(2,1)}), bf16[2,2048,256]{2,1,0:T(8,128)(2,1)}) %all-gather.4.cloned.1.call-update) | async-done | bytes 2097168 | tf_op jit(solution)/shard_map/all_gather | solution.py:127
  79.6 3.2 %convolution_convert_fusion.2 = bf16[256,256]{0,1:T(8,128)(2,1)} fusion(bf16[256,4096]{1,0:T(8,128)(2,1)S(1)} %bitcast.129, bf16[4096,256]{1,0:T(8,128)(2,1)} %bitcast.140), kind=kOutput, calls=%fused_computation.12 | convolution fusion | flops 536936448 | bytes 4325376 | tf_op jit(solution)/shard_map/dot_general | solution.py:108
  82.8 3.4 %all-to-all-start.1 = ((bf16[8,32,256]{2,1,0:T(8,128)(2,1)}), bf16[8,32,256]{2,1,0:T(8,128)(2,1)S(1)}, u32[]{:S(2)}, u32[]{:S(2)}) async-start(bf16[8,32,256]{2,1,0:T(8,128)(2,1)} %bitcast.11), calls=%async_computation.1 | async-start | bytes 262144 | tf_op jit(solution)/shard_map/all_to_all | solution.py:146
  86.2 1.5 %convolution_add_fusion.4 = f32[128,1024]{1,0:T(8,128)S(1)} fusion(f32[128,1024]{1,0:T(8,128)S(1)} %convolution_add_fusion.3, bf16[128,512]{1,0:T(8,128)(2,1)S(1)} %bitcast.135, bf16[1,2,512,1024]{3,2,1,0:T(8,128)(2,1)} %get-tuple-element.7), kind=kOutput, calls=%fused_computation.11 | convolution fusion | flops 134348800 | bytes 2228224 | tf_op jit(solution)/shard_map/dot_general | solution.py:108
  87.7 5.7 %all-to-all-done.1 = bf16[8,32,256]{2,1,0:T(8,128)(2,1)S(1)} async-done(((bf16[8,32,256]{2,1,0:T(8,128)(2,1)}), bf16[8,32,256]{2,1,0:T(8,128)(2,1)S(1)}, u32[]{:S(2)}, u32[]{:S(2)}) %all-to-all-start.1) | async-done | bytes 131104 | tf_op jit(solution)/shard_map/all_to_all | solution.py:146
  93.5 0.3 fusion.22
  93.8 0.3 fusion
  94.3 1.4 %copy-done.5 = bf16[1,2,512,1024]{3,2,1,0:T(8,128)(2,1)S(1)} copy-done((bf16[1,2,512,1024]{3,2,1,0:T(8,128)(2,1)S(1)}, bf16[1,2,512,1024]{3,2,1,0:T(8,128)(2,1)}, u32[]{:S(2)}) %copy-start.5) | copy-done | bytes 2097176
  95.7 0.7 convolution_convert_fusion.1
  96.6 1.4 %copy-done.4 = bf16[1,2,512,1024]{3,2,1,0:T(8,128)(2,1)S(1)} copy-done((bf16[1,2,512,1024]{3,2,1,0:T(8,128)(2,1)S(1)}, bf16[1,2,512,1024]{3,2,1,0:T(8,128)(2,1)}, u32[]{:S(2)}) %copy-start.4) | copy-done | bytes 2097176
  98.0 0.7 convolution_convert_fusion
  98.9 1.4 %copy-done.1 = bf16[1,2,512,1024]{3,2,1,0:T(8,128)(2,1)S(1)} copy-done((bf16[1,2,512,1024]{3,2,1,0:T(8,128)(2,1)S(1)}, bf16[1,2,512,1024]{3,2,1,0:T(8,128)(2,1)}, u32[]{:S(2)}) %copy-start.1) | copy-done | bytes 2097176
  100.3 0.7 convolution_bitcast_fusion
  101.3 12.6 %all_to_all.28 = bf16[16,32,256]{2,1,0:T(8,128)(2,1)S(1)} all-to-all(bf16[16,32,256]{2,1,0:T(8,128)(2,1)S(1)} %bitcast.154), channel_id=1, replica_groups=mesh['pair'=8,'core'=2,'chan'=2] {'pair','core'}, dimensions={0} | all-to-all | bytes 524288 | tf_op jit(solution)/shard_map/all_to_all | solution.py:162
  113.9 1.3 collective-permute-start.1
  115.2 4.5 %collective-permute-start = (bf16[3,256]{1,0:T(4,128)(2,1)S(1)}, bf16[3,256]{1,0:T(4,128)(2,1)S(1)}, u32[]{:S(2)}, u32[]{:S(2)}) collective-permute-start(bf16[3,256]{1,0:T(4,128)(2,1)S(1)} %get-tuple-element.32), channel_id=1, source_target_pairs={{0,1},{2,3},{4,5},{6,7},{8,9},{10,11},{12,13},{14,15},{16,17},{18,... | collective-permute-start | bytes 4616 | tf_op jit(solution)/shard_map/ppermute | solution.py:166
  119.8 1.3 collective-permute-done
  121.1 0.2 fusion.17
  121.4 0.2 fusion.20
  121.6 0.2 fusion.26
  121.8 1.0 copy.54
  (55 shorter events, 1.5 us)
Async XLA Ops:
  6.5 7.9 %copy-start.7 = (s32[4,512]{1,0:T(4,128)S(1)}, s32[4,512]{1,0:T(4,128)}, u32[]{:S(2)}) copy-start(s32[4,512]{1,0:T(4,128)} %param.11) | copy-start | bytes 24580
  6.5 8.5 %copy-start.9 = (f32[2,32,2,2]{1,3,2,0:T(2,128)S(1)}, f32[2,32,2,2]{1,3,2,0:T(2,128)}, u32[]{:S(2)}) copy-start(f32[2,32,2,2]{1,3,2,0:T(2,128)} %param.9) | copy-start | bytes 3076
  6.5 8.8 %copy-start.10 = (f32[256]{0:T(256)S(1)}, f32[256]{0:T(256)}, u32[]{:S(2)}) copy-start(f32[256]{0:T(256)} %param.10) | copy-start | bytes 3076
  6.5 9.4 %copy-start.6 = (f32[4,2,2,512,8]{3,4,2,1,0:T(8,128)S(1)}, f32[4,2,2,512,8]{3,4,2,1,0:T(8,128)}, u32[]{:S(2)}) copy-start(f32[4,2,2,512,8]{3,4,2,1,0:T(8,128)} %param.12) | copy-start | bytes 786436
  6.5 33.2 %all-gather.6.cloned.1.call-start = ((), (), s32[]{:S(2)}) async-start(), calls=%async_computation.4 | async-start | bytes 1310720 | tf_op jit(solution)/shard_map/all_gather | solution.py:128
  10.0 11.3 %all-to-all-start = ((bf16[4,2,16384]{2,1,0:T(2,128)(2,1)}), bf16[4,2,16384]{2,1,0:T(2,128)(2,1)S(1)}, u32[]{:S(2)}, u32[]{:S(2)}) async-start(bf16[4,2,16384]{2,1,0:T(2,128)(2,1)} %reshape.208), calls=%async_computation | async-start | bytes 524288 | tf_op jit(solution)/shard_map/all_to_all | solution.py:126
  14.3 65.3 %all-gather.4.cloned.1.call-start = ((), (), s32[]{:S(2)}) async-start(), calls=%async_computation.3 | async-start | bytes 2359296 | tf_op jit(solution)/shard_map/all_gather | solution.py:127
  23.5 9.2 %copy-start.2 = (bf16[1,2,512,1024]{3,2,1,0:T(8,128)(2,1)S(1)}, bf16[1,2,512,1024]{3,2,1,0:T(8,128)(2,1)}, u32[]{:S(2)}) copy-start(bf16[1,2,512,1024]{3,2,1,0:T(8,128)(2,1)} %get-tuple-element.7) | copy-start | bytes 6291460
  32.4 1.6 %copy-start.3 = (bf16[1,2,512,1024]{3,2,1,0:T(8,128)(2,1)S(1)}, bf16[1,2,512,1024]{3,2,1,0:T(8,128)(2,1)}, u32[]{:S(2)}) copy-start(bf16[1,2,512,1024]{3,2,1,0:T(8,128)(2,1)} %get-tuple-element.8) | copy-start | bytes 6291460
  34.0 2.8 %copy-start = (bf16[3,2,512,1024]{3,2,1,0:T(8,128)(2,1)S(1)}, bf16[3,2,512,1024]{3,2,1,0:T(8,128)(2,1)}, u32[]{:S(2)}) copy-start(bf16[3,2,512,1024]{3,2,1,0:T(8,128)(2,1)} %shard_map.74) | copy-start | bytes 18874372
  82.8 10.7 %all-to-all-start.1 = ((bf16[8,32,256]{2,1,0:T(8,128)(2,1)}), bf16[8,32,256]{2,1,0:T(8,128)(2,1)S(1)}, u32[]{:S(2)}, u32[]{:S(2)}) async-start(bf16[8,32,256]{2,1,0:T(8,128)(2,1)} %bitcast.11), calls=%async_computation.1 | async-start | bytes 262144 | tf_op jit(solution)/shard_map/all_to_all | solution.py:146
  94.1 1.6 %copy-start.5 = (bf16[1,2,512,1024]{3,2,1,0:T(8,128)(2,1)S(1)}, bf16[1,2,512,1024]{3,2,1,0:T(8,128)(2,1)}, u32[]{:S(2)}) copy-start(bf16[1,2,512,1024]{3,2,1,0:T(8,128)(2,1)} %get-tuple-element.9) | copy-start | bytes 6291460
  96.4 1.6 %copy-start.4 = (bf16[1,2,512,1024]{3,2,1,0:T(8,128)(2,1)S(1)}, bf16[1,2,512,1024]{3,2,1,0:T(8,128)(2,1)}, u32[]{:S(2)}) copy-start(bf16[1,2,512,1024]{3,2,1,0:T(8,128)(2,1)} %get-tuple-element.11) | copy-start | bytes 6291460
  98.7 1.6 %copy-start.1 = (bf16[1,2,512,1024]{3,2,1,0:T(8,128)(2,1)S(1)}, bf16[1,2,512,1024]{3,2,1,0:T(8,128)(2,1)}, u32[]{:S(2)}) copy-start(bf16[1,2,512,1024]{3,2,1,0:T(8,128)(2,1)} %get-tuple-element.10) | copy-start | bytes 6291460
  101.2 19.9 %copy-start.8 = (f32[256]{0:T(256)S(1)}, f32[256]{0:T(256)}, u32[]{:S(2)}) copy-start(f32[256]{0:T(256)} %param.13) | copy-start | bytes 3076
  113.9 5.9 %collective-permute-start.1 = (bf16[3,256]{1,0:T(4,128)(2,1)S(1)}, bf16[3,256]{1,0:T(4,128)(2,1)S(1)}, u32[]{:S(2)}, u32[]{:S(2)}) collective-permute-start(bf16[3,256]{1,0:T(4,128)(2,1)S(1)} %get-tuple-element.33), channel_id=1, source_target_pairs={{1,0},{3,2},{5,4},{7,6},{9,8},{11,10},{13,12},{15,14},{17,16},{19,... | collective-permute-start | bytes 4616 | tf_op jit(solution)/shard_map/ppermute | solution.py:167
  115.2 5.8 %collective-permute-start = (bf16[3,256]{1,0:T(4,128)(2,1)S(1)}, bf16[3,256]{1,0:T(4,128)(2,1)S(1)}, u32[]{:S(2)}, u32[]{:S(2)}) collective-permute-start(bf16[3,256]{1,0:T(4,128)(2,1)S(1)} %get-tuple-element.32), channel_id=1, source_target_pairs={{0,1},{2,3},{4,5},{6,7},{8,9},{10,11},{12,13},{14,15},{16,17},{18,... | collective-permute-start | bytes 4616 | tf_op jit(solution)/shard_map/ppermute | solution.py:166
Sparse Core Ops, SparseCore 0:
  8.9 19.4 all-gather.5
  30.5 49.0 all-gather.3
